TPU v7x, 256 devices: a whole 4x4x8 slice. The times are simulated.
256 devices in a mesh: dp: 8 (over z), table: 32 (over y, x, core).
Axes of the slice: x: 4, y: 4, z: 8, core: 2. Of those that a mesh axis runs over, the one named last changes fastest.
Arguments:
- queries: bfloat16 [32768, 2, 512], P(('dp', 'table')), may hold values from -6 to 6
- sub_keys: bfloat16 [2, 2, 512, 256], replicated, may hold values from -0.375 to 0.375
- values: bfloat16 [512, 512, 1024], P('table', None, 'dp'), may hold values from -0.1875 to 0.1875
- slot_first: int32 [32768, 2, 4], P(('dp', 'table')), may hold values from 0 to 511, as said below
- slot_second: int32 [32768, 2, 4], P(('dp', 'table')), may hold values from 0 to 511
- cotangent: bfloat16 [32768, 1024], P(('dp', 'table')), may hold values from -6 to 6
Outputs:
- value_update: float32 [512, 512, 1024], P('table', None, 'dp')
- key_update: float32 [2, 2, 512, 256], P(None, None, ('dp', 'table'))
- clip_factor: float32 [1], replicated
Inputs may be any that keep to these rules, and one draw needn't show every extreme that they name: Within each aligned block of 128 tokens (the tokens of one device), at most 48 of its 1024 slots have slot_first in any one range [r * 16, (r + 1) * 16), and exactly 48 do in one such range.
All inputs are finite; a program needn't handle non-finite values.
Results may differ from a plain program's by a relative error of at most 0.0003.
Values may be sent and summed in bfloat16 or wider, within the bound.
No kernel may reach another device: no remote copies, remote signals or barrier semaphores. Data moves between devices by JAX's collectives and lax.ppermute only.
A program may use at most 64 MiB of HBM per device.

v0:
```python
import math

import jax
import jax.numpy as jnp
from jax import lax
from jax.sharding import Mesh
from jax.sharding import PartitionSpec as P

TABLE = ("table_0", "table_1", "table_2")
DP_TABLE = ("dp", "table_0", "table_1", "table_2")


limit_ratio = 5.0


def from_everyone(shard, axis):
    size = lax.axis_size(axis)
    return lax.all_to_all(
        jnp.broadcast_to(shard[None], (size, *shard.shape)), axis, 0, 0, tiled=True
    )


def in_order(pieces, dim):
    shape = list(pieces.shape[1:])
    shape[dim] *= pieces.shape[0]
    return jnp.moveaxis(pieces, 0, dim).reshape(shape)


def gathered_copies(shard, axis, dim):
    pieces = from_everyone(shard, axis)
    return in_order(pieces, dim)


def of_everyone(shard, axis):
    everything = from_everyone(shard, axis)
    return jnp.sum(everything, axis=0)


def in_blocks(shard, dim, size):
    before, after = (shard.shape[:dim], shard.shape[dim + 1 :])
    return jnp.moveaxis(shard.reshape(*before, size, -1, *after), dim, 0)


def summed_on_arrival(shard, axis, dim):
    size = lax.axis_size(axis)
    pieces = lax.all_to_all(in_blocks(shard, dim, size), axis, 0, 0, tiled=True)
    return jnp.sum(pieces, axis=0)


def sum_in_two_steps(shard, axes, dim):
    far, near = axes
    own = summed_on_arrival(in_blocks(shard, dim, lax.axis_size(far)), near, dim + 1)
    return jnp.sum(lax.all_to_all(own, far, 0, 0, tiled=True), axis=0)


def over_axes(shard, axes):
    far, near = axes
    nearer = of_everyone(shard, near)
    return of_everyone(nearer, far)


def key_terms(dscore, query_half, key_index, key_count):
    labels = jnp.arange(key_count, dtype=jnp.int32)
    weighted = jnp.sum(
        jnp.where(key_index[:, :, :, None] == labels, dscore[:, :, :, None], 0.0), axis=2
    )
    return jnp.einsum(
        "thi,thc->hic", weighted, query_half.astype(jnp.float32), precision=lax.Precision.HIGHEST
    )


def local(queries, sub_keys, values, slot_first, slot_second, cotangent):
    table_size = lax.axis_size(TABLE)
    data_size = lax.axis_size("dp")
    token_count = slot_first.shape[0]
    head_count = slot_first.shape[1]
    pick_count = slot_first.shape[2]
    half_width = queries.shape[2] // 2
    key_count = sub_keys.shape[2]
    first_block = values.shape[0]
    column_count = values.shape[2]
    slot_count = token_count * head_count * pick_count
    capacity = 3 * slot_count // (2 * table_size)
    head_ids = jnp.arange(head_count, dtype=jnp.int32)[None, :, None]
    query_first = queries[:, :, :half_width]
    query_second = queries[:, :, half_width:]
    key_first = sub_keys[0][head_ids, slot_first]
    key_second = sub_keys[1][head_ids, slot_second]
    raw_score = jnp.einsum(
        "thc,thkc->thk", query_first, key_first, preferred_element_type=jnp.float32
    )
    raw_score = raw_score + jnp.einsum(
        "thc,thkc->thk", query_second, key_second, preferred_element_type=jnp.float32
    )
    exp_score = jnp.exp(raw_score)
    weight = exp_score / jnp.sum(exp_score, axis=2, keepdims=True)
    owner_group = (slot_first // first_block).reshape(slot_count)
    local_row = (slot_first % first_block * key_count + slot_second).reshape(slot_count)
    token_row = jnp.broadcast_to(
        jnp.arange(token_count, dtype=jnp.int32)[:, None, None], slot_first.shape
    ).reshape(slot_count)
    member = (owner_group[:, None] == jnp.arange(table_size, dtype=jnp.int32)[None, :]).astype(
        jnp.int32
    )
    before = jnp.sum((jnp.cumsum(member, axis=0) - member) * member, axis=1)
    target = owner_group * capacity + before
    send_rows = (
        jnp.zeros((table_size * capacity,), jnp.int32)
        .at[target]
        .set(local_row)
        .reshape(table_size, capacity)
    )
    send_weight = (
        jnp.zeros((table_size * capacity,), jnp.float32)
        .at[target]
        .set(weight.reshape(slot_count))
        .reshape(table_size, capacity)
    )
    send_token = (
        jnp.zeros((table_size * capacity,), jnp.int32)
        .at[target]
        .set(token_row)
        .reshape(table_size, capacity)
    )
    cot_columns = lax.all_to_all(cotangent, "dp", split_axis=1, concat_axis=0, tiled=True)
    cot_all = lax.all_gather(cot_columns, TABLE, axis=0, tiled=True)
    received = (
        lax.all_to_all(send_rows, TABLE, split_axis=0, concat_axis=0, tiled=True),
        lax.all_to_all(send_weight, TABLE, split_axis=0, concat_axis=0, tiled=True),
        lax.all_to_all(send_token, TABLE, split_axis=0, concat_axis=0, tiled=True),
    )
    rows_all, weight_all, token_all = (
        gathered_copies(received[0], "dp", 0),
        gathered_copies(received[1], "dp", 0),
        gathered_copies(received[2], "dp", 0),
    )
    source_index = jnp.arange(data_size * table_size, dtype=jnp.int32)[:, None]
    position = (
        source_index % table_size * data_size + source_index // table_size
    ) * token_count + token_all
    table_flat = values.reshape(first_block * key_count, column_count)
    rows_flat = rows_all.reshape(-1)
    weight_flat = weight_all.reshape(-1)
    cot_part = cot_all[position.reshape(-1)]
    value_part = table_flat[rows_flat]
    partial_dots = jnp.einsum("rc,rc->r", cot_part, value_part, preferred_element_type=jnp.float32)
    start = jnp.zeros((first_block * key_count, column_count), jnp.float32)
    value_grad = start.at[rows_flat].add(weight_flat[:, None] * cot_part.astype(jnp.float32))
    partial_dots = partial_dots.reshape(data_size, table_size, capacity)
    summed = of_everyone(partial_dots, "dp")
    own_share = lax.dynamic_index_in_dim(summed, lax.axis_index("dp"), 0, keepdims=False)
    returned = lax.all_to_all(own_share, TABLE, split_axis=0, concat_axis=0, tiled=True)
    picked = returned.reshape(table_size * capacity)[target].reshape(
        token_count, head_count, pick_count
    )
    dscore = weight * (picked - jnp.sum(weight * picked, axis=2, keepdims=True))
    key_grad = jnp.stack(
        [
            key_terms(dscore, query_first, slot_first, key_count),
            key_terms(dscore, query_second, slot_second, key_count),
        ]
    )
    value_sq = jnp.sum(value_grad * value_grad)
    key_part = sum_in_two_steps(key_grad, (("dp", "table_0"), ("table_1", "table_2")), 2)
    local_sq = value_sq + jnp.sum(key_part * key_part)
    total_sq = over_axes(local_sq, (("dp", "table_0"), ("table_1", "table_2")))
    all_tokens = token_count * data_size * table_size
    clip_factor = jnp.minimum(1.0, limit_ratio * math.sqrt(all_tokens) / jnp.sqrt(total_sq))
    value_update = (clip_factor * value_grad).reshape(first_block, key_count, column_count)
    key_update = clip_factor * key_part
    return (value_update, key_update, clip_factor.reshape(1))


def solution(mesh):
    torus = Mesh(
        mesh.devices.reshape(mesh.shape["dp"], 4, 4, 2), ("dp", "table_0", "table_1", "table_2")
    )
    return jax.shard_map(
        local,
        mesh=torus,
        in_specs=(
            P(DP_TABLE, None, None),
            P(),
            P(TABLE, None, "dp"),
            P(DP_TABLE, None, None),
            P(DP_TABLE, None, None),
            P(DP_TABLE, None),
        ),
        out_specs=(P(TABLE, None, "dp"), P(None, None, DP_TABLE, None), P()),
        check_vma=False,
    )
```

profile of v0, /device:TPU:1, one launch (start us, length us, event | category | flops | bytes accessed | tf_op | source)
XLA Modules:
  0.0 444.2 jit_solution(7563957080121406544)
XLA Ops:
  8.4 19.4 %all_to_all.97 = bf16[128,8,128]{2,0,1:T(8,128)(2,1)} all-to-all(bf16[128,8,128]{2,0,1:T(8,128)(2,1)S(1)} %copy_bitcast_fusion), channel_id=1, replica_groups=mesh['dp'=8,'table_0'=4,'table_1'=4,'table_2'=2] {'dp'}, dimensions={1} | all-to-all | bytes 524288 | tf_op jit(solution)/shard_map/all_to_all | solution.py:125
  29.5 9.0 %reduce-window.6 = s32[32,8,128]{2,1,0:T(8,128)S(1)} reduce-window(s32[32,8,128]{2,1,0:T(8,128)S(1)} %fusion.11, s32[]{:T(128)} %constant.81.clone.1), window={size=1x1x128 pad=0_0x0_0x127_0}, to_apply=%region_0.0 | reduce-window | flops 4161536 | bytes 262148 | tf_op jit(solution)/shard_map/reduce-window
  39.4 4.3 scatter_custom_fusion
  44.4 9.5 %all-to-all-start = ((s32[32,1,48]{2,1,0:T(1,128)}), s32[32,1,48]{2,1,0:T(1,128)}, u32[]{:S(2)}, u32[]{:S(2)}) async-start(s32[32,1,48]{2,1,0:T(1,128)} %all_to_all.64), calls=%async_computation | async-start | bytes 32768 | tf_op jit(solution)/shard_map/all_to_all | solution.py:128
  56.6 4.3 scatter_custom_fusion.2
  61.6 7.4 %all-to-all-start.5 = ((s32[32,1,48]{2,1,0:T(1,128)}), s32[32,1,48]{2,1,0:T(1,128)}, u32[]{:S(2)}, u32[]{:S(2)}) async-start(s32[32,1,48]{2,1,0:T(1,128)} %all_to_all.74), calls=%async_computation.5 | async-start | bytes 32768 | tf_op jit(solution)/shard_map/all_to_all | solution.py:130
  70.6 5.6 %all-to-all-done.5 = s32[32,1,48]{2,1,0:T(1,128)} async-done(((s32[32,1,48]{2,1,0:T(1,128)}), s32[32,1,48]{2,1,0:T(1,128)}, u32[]{:S(2)}, u32[]{:S(2)}) %all-to-all-start.5) | async-done | bytes 6176 | tf_op jit(solution)/shard_map/all_to_all | solution.py:130
  76.2 4.0 all-to-all-start.1
  82.2 5.0 %all-to-all-done.1 = s32[8,1,1536]{2,1,0:T(1,128)} async-done(((s32[8,1,1536]{2,1,0:T(1,128)}), s32[8,1,1536]{2,1,0:T(1,128)}, u32[]{:S(2)}, u32[]{:S(2)}) %all-to-all-start.1) | async-done | bytes 49184 | tf_op jit(solution)/shard_map/all_to_all | solution.py:18
  87.3 4.1 all-to-all-start.6
  92.6 10.7 %gather_fusion = bf16[1024,256]{1,0:T(8,128)(2,1)} fusion(bf16[2,512,256]{2,1,0:T(8,128)(2,1)S(1)} %get-tuple-element.8, s32[1024]{0:T(1024)S(1)} %reshape.253), kind=kCustom, calls=%fused_computation | custom fusion | bytes 1056768 | tf_op jit(solution)/shard_map/gather | solution.py:87
  105.6 5.8 %gather_fusion.1 = bf16[1024,256]{1,0:T(8,128)(2,1)S(1)} fusion(bf16[2,512,256]{2,1,0:T(8,128)(2,1)S(1)} %get-tuple-element.7, s32[1024]{0:T(1024)S(1)} %reshape.259), kind=kCustom, calls=%fused_computation.1 | custom fusion | bytes 1056768 | tf_op jit(solution)/shard_map/gather | solution.py:88
  117.3 43.7 %gather_fusion.3 = bf16[12288,128]{1,0:T(8,128)(2,1)} fusion(bf16[8192,128]{1,0:T(8,128)(2,1)S(1)} %bitcast.72, s32[12288]{0:T(1024)S(1)} %broadcast_clamp_fusion), kind=kCustom, calls=%fused_computation.3 | custom fusion | bytes 6340608 | tf_op jit(solution)/shard_map/gather | solution.py:145
  161.1 45.9 %gather_fusion.2 = bf16[12288,128]{1,0:T(8,128)(2,1)} fusion(bf16[32768,128]{1,0:T(8,128)(2,1)} %all-gather.2.cloned.1.call-done, s32[12288]{0:T(1024)S(1)} %broadcast_clamp_fusion.1), kind=kCustom, calls=%fused_computation.2 | custom fusion | bytes 6340608 | tf_op jit(solution)/shard_map/gather | solution.py:144
  207.0 3.7 fusion.1
  212.7 6.5 %all-to-all-start.7 = ((f32[8,1,12288]{2,1,0:T(1,128)}), f32[8,1,12288]{2,1,0:T(1,128)S(1)}, u32[]{:S(2)}, u32[]{:S(2)}) async-start(f32[8,1,12288]{2,1,0:T(1,128)} %reshape.361), calls=%async_computation.7 | async-start | bytes 786432 | tf_op jit(solution)/shard_map/all_to_all | solution.py:18
  222.4 8.9 %all-to-all-done.7 = f32[8,1,12288]{2,1,0:T(1,128)S(1)} async-done(((f32[8,1,12288]{2,1,0:T(1,128)}), f32[8,1,12288]{2,1,0:T(1,128)S(1)}, u32[]{:S(2)}, u32[]{:S(2)}) %all-to-all-start.7) | async-done | bytes 393248 | tf_op jit(solution)/shard_map/all_to_all | solution.py:18
  234.6 7.0 %all-to-all-start.8 = ((f32[32,1,48]{2,1,0:T(1,128)}), f32[32,1,48]{2,1,0:T(1,128)S(1)}, u32[]{:S(2)}, u32[]{:S(2)}) async-start(f32[32,1,48]{2,1,0:T(1,128)} %bitcast.22), calls=%async_computation.8 | async-start | bytes 32768 | tf_op jit(solution)/shard_map/all_to_all | solution.py:152
  241.6 7.0 %all-to-all-done.8 = f32[32,1,48]{2,1,0:T(1,128)S(1)} async-done(((f32[32,1,48]{2,1,0:T(1,128)}), f32[32,1,48]{2,1,0:T(1,128)S(1)}, u32[]{:S(2)}, u32[]{:S(2)}) %all-to-all-start.8) | async-done | bytes 6176 | tf_op jit(solution)/shard_map/all_to_all | solution.py:152
  249.9 6.1 %gather_fusion.4 = f32[1024]{0:T(1024)S(1)} fusion(f32[1536]{0:T(1024)S(1)} %reshape.248, s32[1024]{0:T(1024)S(1)} %broadcast_clamp_fusion.2), kind=kCustom, calls=%fused_computation.4 | custom fusion | bytes 12288 | tf_op jit(solution)/shard_map/gather | solution.py:153
  256.9 4.3 scatter_custom_fusion.1
  261.9 4.3 all-to-all-start.2
  273.3 4.9 %all-to-all-start.9 = ((f32[8,32,2,2,2,256]{5,4,1,3,2,0:T(2,128)}), f32[8,32,2,2,2,256]{5,4,1,3,2,0:T(2,128)}, u32[]{:S(2)}, u32[]{:S(2)}) async-start(f32[8,32,2,2,2,256]{5,4,1,3,2,0:T(2,128)} %copy.111), calls=%async_computation.9 | async-start | bytes 4194304 | tf_op jit(solution)/shard_map/all_to_all | solution.py:46
  279.0 25.6 %all-to-all-done.9 = f32[8,32,2,2,2,256]{5,4,1,3,2,0:T(2,128)} async-done(((f32[8,32,2,2,2,256]{5,4,1,3,2,0:T(2,128)}), f32[8,32,2,2,2,256]{5,4,1,3,2,0:T(2,128)}, u32[]{:S(2)}, u32[]{:S(2)}) %all-to-all-start.9) | async-done | bytes 2097184 | tf_op jit(solution)/shard_map/all_to_all | solution.py:46
  304.5 3.3 all-to-all-start.3
  311.1 3.7 all-to-all-done.3
  314.8 5.2 %all-to-all-start.10 = ((f32[32,2,2,2,256]{4,3,2,1,0:T(2,128)}), f32[32,2,2,2,256]{4,3,2,1,0:T(2,128)S(1)}, u32[]{:S(2)}, u32[]{:S(2)}) async-start(f32[32,2,2,2,256]{4,3,2,1,0:T(2,128)} %copy.113), calls=%async_computation.10 | async-start | bytes 524288 | tf_op jit(solution)/shard_map/all_to_all | solution.py:53
  321.1 75.1 %scatter_custom_fusion.3 = f32[8192,128]{1,0:T(8,128)} fusion(s32[12288]{0:T(1024)} %bitcast.80, bf16[12288,128]{1,0:T(8,128)(2,1)} %gather_fusion.2, f32[12288]{0:T(1024)S(1)} %mul.83, f32[]{:T(128)} %constant.80.clone.1), kind=kCustom, calls=%fused_computation.11 | custom fusion | flops 4718592 | bytes 7389696 | tf_op jit(solution)/shard_map/scatter-add | solution.py:148
  396.1 3.9 multiply_reduce_fusion
  402.0 8.4 %all_to_all.98 = f32[8,1,1]{2,1,0:T(1,128)S(1)} all-to-all(f32[8,1,1]{2,1,0:T(1,128)S(1)} %broadcast_in_dim.122), channel_id=1, replica_groups=mesh['dp'=8,'table_0'=4,'table_1'=4,'table_2'=2] {'table_1','table_2'}, dimensions={0} | all-to-all | bytes 64 | tf_op jit(solution)/shard_map/all_to_all | solution.py:18
  411.7 18.1 %all_to_all.99 = f32[32,1,1]{2,1,0:T(1,128)S(1)} all-to-all(f32[32,1,1]{2,1,0:T(1,128)S(1)} %broadcast_in_dim.123), channel_id=1, replica_groups=mesh['dp'=8,'table_0'=4,'table_1'=4,'table_2'=2] {'dp','table_0'}, dimensions={0} | all-to-all | bytes 256 | tf_op jit(solution)/shard_map/all_to_all | solution.py:18
  431.1 4.5 %broadcast_multiply_fusion = f32[8192,128]{1,0:T(8,128)} fusion(f32[8192,128]{1,0:T(8,128)} %scatter_custom_fusion.3, f32[]{:T(128)} %min_shard_map.3), kind=kLoop, calls=%fused_computation.16 | loop fusion | flops 1048576 | bytes 8388612 | tf_op jit(solution)/shard_map/mul | solution.py:169
  (125 shorter events, 47.1 us)
Async XLA Ops:
  7.2 110.1 %copy-start = (bf16[16,512,128]{2,1,0:T(8,128)(2,1)S(1)}, bf16[16,512,128]{2,1,0:T(8,128)(2,1)}, u32[]{:S(2)}) copy-start(bf16[16,512,128]{2,1,0:T(8,128)(2,1)} %param.8) | copy-start | bytes 6291460
  7.2 153.9 %all-gather.2.cloned.1.call-start = ((), (), s32[]{:S(2)}) async-start(), calls=%async_computation.13 | async-start | bytes 8650752 | tf_op jit(solution)/shard_map/all_gather | solution.py:126
  8.4 60.7 %copy-start.8 = (s32[128,2,4]{0,2,1:T(4,128)S(1)}, s32[128,2,4]{0,2,1:T(4,128)}, u32[]{:S(2)}) copy-start(s32[128,2,4]{0,2,1:T(4,128)} %param.9) | copy-start | bytes 12292
  8.4 71.8 %copy-start.9 = (s32[128,2,4]{0,2,1:T(4,128)S(1)}, s32[128,2,4]{0,2,1:T(4,128)}, u32[]{:S(2)}) copy-start(s32[128,2,4]{0,2,1:T(4,128)} %param.10) | copy-start | bytes 12292
  44.4 17.2 %all-to-all-start = ((s32[32,1,48]{2,1,0:T(1,128)}), s32[32,1,48]{2,1,0:T(1,128)}, u32[]{:S(2)}, u32[]{:S(2)}) async-start(s32[32,1,48]{2,1,0:T(1,128)} %all_to_all.64), calls=%async_computation | async-start | bytes 32768 | tf_op jit(solution)/shard_map/all_to_all | solution.py:128
  56.3 162.9 %copy-start.1 = (bf16[128,2,256]{2,1,0:T(2,128)(2,1)}, bf16[128,2,256]{2,1,0:T(2,128)(2,1)S(1)}, u32[]{:S(2)}) copy-start(bf16[128,2,256]{2,1,0:T(2,128)(2,1)S(1)} %get-tuple-element.10) | copy-start | bytes 393220
  56.3 162.9 %copy-start.3 = (bf16[128,2,256]{2,1,0:T(2,128)(2,1)}, bf16[128,2,256]{2,1,0:T(2,128)(2,1)S(1)}, u32[]{:S(2)}) copy-start(bf16[128,2,256]{2,1,0:T(2,128)(2,1)S(1)} %get-tuple-element.9) | copy-start | bytes 393220
  61.6 14.6 %all-to-all-start.5 = ((s32[32,1,48]{2,1,0:T(1,128)}), s32[32,1,48]{2,1,0:T(1,128)}, u32[]{:S(2)}, u32[]{:S(2)}) async-start(s32[32,1,48]{2,1,0:T(1,128)} %all_to_all.74), calls=%async_computation.5 | async-start | bytes 32768 | tf_op jit(solution)/shard_map/all_to_all | solution.py:130
  76.2 11.1 %all-to-all-start.1 = ((s32[8,1,1536]{2,1,0:T(1,128)}), s32[8,1,1536]{2,1,0:T(1,128)}, u32[]{:S(2)}, u32[]{:S(2)}) async-start(s32[8,1,1536]{2,1,0:T(1,128)} %reshape.355), calls=%async_computation.1 | async-start | bytes 98304 | tf_op jit(solution)/shard_map/all_to_all | solution.py:18
  87.3 27.5 %all-to-all-start.6 = ((s32[8,1,1536]{2,1,0:T(1,128)}), s32[8,1,1536]{2,1,0:T(1,128)}, u32[]{:S(2)}, u32[]{:S(2)}) async-start(s32[8,1,1536]{2,1,0:T(1,128)} %reshape.357), calls=%async_computation.6 | async-start | bytes 98304 | tf_op jit(solution)/shard_map/all_to_all | solution.py:18
  92.6 12.6 %copy-start.10 = (s32[128,2,4,1]{0,2,1,3:T(4,128)S(1)}, s32[128,2,4,1]{0,2,1,3:T(4,128)}, u32[]{:S(2)}) copy-start(s32[128,2,4,1]{0,2,1,3:T(4,128)} %fusion.27) | copy-start | bytes 12292
  116.6 0.6 copy-start.6
  117.2 43.7 %copy-start.7 = (s32[12288,1]{0,1:T(1,128)S(1)}, s32[12288,1]{0,1:T(1,128)}, u32[]{:S(2)}) copy-start(s32[12288,1]{0,1:T(1,128)} %add.131) | copy-start | bytes 147460
  212.7 8.6 %copy-start.5 = (bf16[128,2,4,256]{3,2,1,0:T(4,128)(2,1)S(1)}, bf16[128,2,4,256]{3,2,1,0:T(4,128)(2,1)}, u32[]{:S(2)}) copy-start(bf16[128,2,4,256]{3,2,1,0:T(4,128)(2,1)} %reshape.262) | copy-start | bytes 1572868
  212.7 18.6 %all-to-all-start.7 = ((f32[8,1,12288]{2,1,0:T(1,128)}), f32[8,1,12288]{2,1,0:T(1,128)S(1)}, u32[]{:S(2)}, u32[]{:S(2)}) async-start(f32[8,1,12288]{2,1,0:T(1,128)} %reshape.361), calls=%async_computation.7 | async-start | bytes 786432 | tf_op jit(solution)/shard_map/all_to_all | solution.py:18
  233.8 22.5 %copy-start.11 = (f32[128,2,1,4]{3,2,1,0:T(1,128)S(1)}, f32[128,2,1,4]{3,2,1,0:T(1,128)}, u32[]{:S(2)}) copy-start(f32[128,2,1,4]{3,2,1,0:T(1,128)} %fusion.6) | copy-start | bytes 12292
  233.8 22.5 %copy-start.12 = (f32[128,2,1,4]{3,2,1,0:T(1,128)S(1)}, f32[128,2,1,4]{3,2,1,0:T(1,128)}, u32[]{:S(2)}) copy-start(f32[128,2,1,4]{3,2,1,0:T(1,128)} %fusion.4) | copy-start | bytes 12292
  234.6 14.0 %all-to-all-start.8 = ((f32[32,1,48]{2,1,0:T(1,128)}), f32[32,1,48]{2,1,0:T(1,128)S(1)}, u32[]{:S(2)}, u32[]{:S(2)}) async-start(f32[32,1,48]{2,1,0:T(1,128)} %bitcast.22), calls=%async_computation.8 | async-start | bytes 32768 | tf_op jit(solution)/shard_map/all_to_all | solution.py:152
  256.0 11.2 %copy-start.4 = (bf16[128,2,256]{2,1,0:T(2,128)(2,1)S(1)}, bf16[128,2,256]{2,1,0:T(2,128)(2,1)}, u32[]{:S(2)}) copy-start(bf16[128,2,256]{2,1,0:T(2,128)(2,1)} %copy-done.3) | copy-start | bytes 393220
  256.7 11.8 %copy-start.2 = (bf16[128,2,256]{2,1,0:T(2,128)(2,1)S(1)}, bf16[128,2,256]{2,1,0:T(2,128)(2,1)}, u32[]{:S(2)}) copy-start(bf16[128,2,256]{2,1,0:T(2,128)(2,1)} %copy-done.1) | copy-start | bytes 393220
  261.9 11.4 %all-to-all-start.2 = ((f32[32,1,48]{2,1,0:T(1,128)}), f32[32,1,48]{2,1,0:T(1,128)S(1)}, u32[]{:S(2)}, u32[]{:S(2)}) async-start(f32[32,1,48]{2,1,0:T(1,128)} %all_to_all.67), calls=%async_computation.2 | async-start | bytes 32768 | tf_op jit(solution)/shard_map/all_to_all | solution.py:129
  273.3 31.2 %all-to-all-start.9 = ((f32[8,32,2,2,2,256]{5,4,1,3,2,0:T(2,128)}), f32[8,32,2,2,2,256]{5,4,1,3,2,0:T(2,128)}, u32[]{:S(2)}, u32[]{:S(2)}) async-start(f32[8,32,2,2,2,256]{5,4,1,3,2,0:T(2,128)} %copy.111), calls=%async_computation.9 | async-start | bytes 4194304 | tf_op jit(solution)/shard_map/all_to_all | solution.py:46
  304.5 10.3 %all-to-all-start.3 = ((f32[8,1,1536]{2,1,0:T(1,128)}), f32[8,1,1536]{2,1,0:T(1,128)S(1)}, u32[]{:S(2)}, u32[]{:S(2)}) async-start(f32[8,1,1536]{2,1,0:T(1,128)} %reshape.359), calls=%async_computation.3 | async-start | bytes 98304 | tf_op jit(solution)/shard_map/all_to_all | solution.py:18
  314.8 85.2 %all-to-all-start.10 = ((f32[32,2,2,2,256]{4,3,2,1,0:T(2,128)}), f32[32,2,2,2,256]{4,3,2,1,0:T(2,128)S(1)}, u32[]{:S(2)}, u32[]{:S(2)}) async-start(f32[32,2,2,2,256]{4,3,2,1,0:T(2,128)} %copy.113), calls=%async_computation.10 | async-start | bytes 524288 | tf_op jit(solution)/shard_map/all_to_all | solution.py:53
Sparse Core Ops, SparseCore 0:
  27.9 56.3 all-gather.1
where the time goes:
time: 446 us; the launch traced here: 444 us
  local copies, waits for them, and re-layouts  153 us (34%)
  other arithmetic  111 us (25%)
  starting transfers between devices  56.3 us (13%)
  waiting for transfers between devices  56.3 us (13%)
  blocking collectives  45.9 us (10%)
  between operations  17.8 us (4%)
    scatter-add x1, other arithmetic, local(): start.at[rows_flat].add(weight_flat[:, None] * cot_part.astype(jnp.float32))  75.1 us
    gather x1, local copies, waits for them, and re-layouts, local(): cot_part = cot_all[position.reshape(-1)]  45.9 us
    gather x1, local copies, waits for them, and re-layouts, local(): value_part = table_flat[rows_flat]  43.7 us
    all_to_all x2, blocking collectives, from_everyone(): lax.all_to_all(jnp.broadcast_to(shard[None], (size, *shard.shape)), axis,...  26.5 us
    all_to_all x1, waiting for transfers between devices, summed_on_arrival(): pieces = lax.all_to_all(in_blocks(shard, dim, size), axis, 0, 0, tiled=True)  25.6 us
    all_to_all x1, blocking collectives, local(): lax.all_to_all(cotangent, 'dp', split_axis=1, concat_axis=0, tiled=True)  19.4 us
    all_to_all x4, starting transfers between devices, from_everyone(): lax.all_to_all(jnp.broadcast_to(shard[None], (size, *shard.shape)), axis,...  17.9 us
    all_to_all x4, waiting for transfers between devices, from_everyone(): lax.all_to_all(jnp.broadcast_to(shard[None], (size, *shard.shape)), axis,...  17.6 us
  transfers between devices with their start and end apart: 11, of which 7 were waited for; matrix products, arithmetic and copies ran while one was open for 43% of the time, Pallas kernels for 0%

commit v1 on v0

v1 whole, which is shorter than its diff:
```python
import math

import jax
import jax.numpy as jnp
from jax import lax
from jax.experimental import pallas as pl
from jax.experimental.pallas import tpu as pltpu
from jax.sharding import Mesh
from jax.sharding import PartitionSpec as P

TABLE = ("table_0", "table_1", "table_2")
DP_TABLE = ("dp", "table_0", "table_1", "table_2")
ALL = ("dp", "table_0", "table_1", "table_2")
NSUB = 512
BLK = 16
CAP = 48
OWN = 32
NDP = 8
TOK = 128
PICKS = 8
HALF = 256
KEYS = NSUB // NDP
LISTS = OWN * NDP
ROWS = BLK * NSUB
ACCS = 4
F32 = jnp.float32
BF16 = jnp.bfloat16
LIMIT_RATIO = 5.0

NT = (((1,), (1,)), ((), ()))
NN = (((1,), (0,)), ((), ()))


def pieces(x):
    high = x.astype(BF16)
    rest = x - high.astype(F32)
    mid = rest.astype(BF16)
    low = (rest - mid.astype(F32)).astype(BF16)
    return high, mid, low


def prep_kernel(q_ref, keys_ref, first_ref, second_ref, rec_ref, aux_ref):
    first = first_ref[...]
    second = second_ref[...]
    key_id = lax.broadcasted_iota(jnp.int32, (NSUB, TOK), 0)
    scores = [None] * PICKS
    for half, index in ((0, first), (1, second)):
        for head in range(2):
            at = head * 2 * HALF + half * HALF
            table = lax.dot_general(
                keys_ref[half, head], q_ref[:, at : at + HALF], NT, preferred_element_type=F32
            )
            for k in range(4):
                slot = head * 4 + k
                part = jnp.sum(
                    jnp.where(key_id == index[slot : slot + 1, :], table, 0.0),
                    axis=0,
                    keepdims=True,
                )
                scores[slot] = part if scores[slot] is None else scores[slot] + part
    exps = [jnp.exp(s) for s in scores]
    weights = []
    for head in range(2):
        e = exps[head * 4 : head * 4 + 4]
        total = (e[0] + e[1]) + (e[2] + e[3])
        weights += [x / total for x in e]
    owner = jnp.right_shift(first, 4)
    owner_id = lax.broadcasted_iota(jnp.int32, (OWN, TOK), 0)
    member = [
        jnp.where(owner_id == owner[s : s + 1, :], 1.0, 0.0).astype(F32) for s in range(PICKS)
    ]
    earlier = jnp.where(
        lax.broadcasted_iota(jnp.int32, (TOK, TOK), 0)
        < lax.broadcasted_iota(jnp.int32, (TOK, TOK), 1),
        1.0,
        0.0,
    ).astype(BF16)
    member_all = jnp.concatenate(member, axis=0).astype(BF16)
    ranks = lax.dot_general(member_all, earlier, NN, preferred_element_type=F32)
    base = jnp.zeros((OWN, 1), F32)
    token = lax.broadcasted_iota(jnp.int32, (1, TOK), 1)
    lane_id = lax.broadcasted_iota(jnp.int32, (TOK, TOK), 0)
    record = jnp.zeros((OWN, TOK), F32)
    targets = []
    for s in range(PICKS):
        rank = jnp.sum(
            member[s] * (ranks[s * OWN : (s + 1) * OWN, :] + base), axis=0, keepdims=True
        )
        base = base + jnp.sum(member[s], axis=1, keepdims=True)
        place = rank.astype(jnp.int32)
        code = (
            (jnp.bitwise_and(first[s : s + 1, :], BLK - 1) * NSUB + second[s : s + 1, :]) * TOK
            + token
        ).astype(F32)
        entry = jnp.where(lane_id == place, code, 0.0) + jnp.where(
            lane_id == place + CAP, weights[s], 0.0
        )
        for piece in pieces(entry):
            record = record + lax.dot_general(
                member[s].astype(BF16), piece, NT, preferred_element_type=F32
            )
        targets.append((owner[s : s + 1, :] * TOK + place).astype(F32))
    lane = lax.broadcasted_iota(jnp.int32, (OWN, TOK), 1)
    rec_ref[...] = jnp.where(lane == 2 * CAP, base, record)
    aux_ref[0:8, :] = jnp.concatenate(weights, axis=0)
    aux_ref[8:16, :] = jnp.concatenate(targets, axis=0)
    aux_ref[16:24, :] = first.astype(F32)
    aux_ref[24:32, :] = second.astype(F32)


def prep(q, keys, first, second):
    return pl.pallas_call(
        prep_kernel,
        out_shape=(
            jax.ShapeDtypeStruct((OWN, TOK), F32),
            jax.ShapeDtypeStruct((32, TOK), F32),
        ),
        name="prep",
    )(q, keys, first, second)


def expand_kernel(rec_ref, cot_ref, out_ref):
    record = rec_ref[0]
    square = jnp.concatenate([record, record, record, record], axis=0)
    columns = jnp.transpose(square)
    token = jnp.bitwise_and(columns[0:CAP, :].astype(jnp.int32), TOK - 1)
    lane = lax.broadcasted_iota(jnp.int32, (CAP, TOK), 1)
    cot = cot_ref[0]
    for o in range(OWN):
        chosen = jnp.where(token[:, o : o + 1] == lane, 1.0, 0.0).astype(BF16)
        out_ref[o, 0] = lax.dot_general(
            chosen, cot, NN, preferred_element_type=F32
        ).astype(BF16)


def expand(records, cot):
    return pl.pallas_call(
        expand_kernel,
        grid=(NDP,),
        in_specs=[
            pl.BlockSpec((1, OWN, TOK), lambda s: (s, 0, 0)),
            pl.BlockSpec((1, TOK, TOK), lambda s: (s, 0, 0)),
        ],
        out_specs=pl.BlockSpec((OWN, 1, CAP, TOK), lambda s: (0, s, 0, 0)),
        out_shape=jax.ShapeDtypeStruct((OWN, NDP, CAP, TOK), BF16),
        name="expand",
    )(records, cot)


GATHER_LISTS = 16


def gather_kernel(row_ref, table_ref, out_ref, wide_ref, got_ref):
    step = pl.program_id(0)

    @pl.when(step == 0)
    def _():
        def widen(i, carry):
            at = pl.multiple_of(i * 256, 256)
            wide_ref[pl.ds(at, 256), :] = table_ref[pl.ds(at, 256), :].astype(F32)
            return carry

        lax.fori_loop(0, ROWS // 256, widen, 0)

    def one_list(i, carry):
        for j in range(CAP):
            row = row_ref[step * GATHER_LISTS + i, j]
            got_ref[pl.ds(i * CAP + j, 1), :] = wide_ref[pl.ds(row, 1), :]
        return carry

    lax.fori_loop(0, GATHER_LISTS, one_list, 0)
    out_ref[...] = got_ref[...].astype(BF16)


def gather_rows(row, table):
    return pl.pallas_call(
        gather_kernel,
        grid=(LISTS // GATHER_LISTS,),
        in_specs=[
            pl.BlockSpec(memory_space=pltpu.SMEM),
            pl.BlockSpec((ROWS, TOK), lambda g: (0, 0)),
        ],
        out_specs=pl.BlockSpec((GATHER_LISTS * CAP, TOK), lambda g: (g, 0)),
        out_shape=jax.ShapeDtypeStruct((LISTS * CAP, TOK), BF16),
        scratch_shapes=[
            pltpu.VMEM((ROWS, TOK), F32),
            pltpu.VMEM((GATHER_LISTS * CAP, TOK), F32),
        ],
        cost_estimate=pl.CostEstimate(
            flops=20_000_000_000, transcendentals=0, bytes_accessed=6_000_000
        ),
        name="gather_rows",
    )(row, table)


DOT_LISTS = 32


def dots_kernel(cot_ref, value_ref, out_ref):
    place = lax.broadcasted_iota(jnp.int32, (CAP, TOK), 0)
    lane = lax.broadcasted_iota(jnp.int32, (CAP, TOK), 1)
    own = place == lane
    for i in range(DOT_LISTS):
        at = i * CAP
        product = cot_ref[at : at + CAP, :].astype(F32) * value_ref[at : at + CAP, :].astype(F32)
        total = jnp.sum(product, axis=1, keepdims=True)
        out_ref[i : i + 1, :] = jnp.sum(jnp.where(own, total, 0.0), axis=0, keepdims=True)


def dots(cot, value):
    return pl.pallas_call(
        dots_kernel,
        grid=(LISTS // DOT_LISTS,),
        in_specs=[
            pl.BlockSpec((DOT_LISTS * CAP, TOK), lambda g: (g, 0)),
            pl.BlockSpec((DOT_LISTS * CAP, TOK), lambda g: (g, 0)),
        ],
        out_specs=pl.BlockSpec((DOT_LISTS, TOK), lambda g: (g, 0)),
        out_shape=jax.ShapeDtypeStruct((LISTS, TOK), F32),
        name="dots",
    )(cot, value)


SCATTER_LISTS = 8


def scatter_kernel(row_ref, rec_ref, cot_ref, out_ref, sq_ref, wide_ref, *accs):
    step = pl.program_id(0)

    @pl.when(step == 0)
    def _():
        def clear(i, carry):
            at = pl.multiple_of(i * 64, 64)
            for acc in accs:
                acc[pl.ds(at, 64), :] = jnp.zeros((64, TOK), F32)
            return carry

        lax.fori_loop(0, ROWS // 64, clear, 0)

    wide_ref[...] = cot_ref[...].astype(F32)

    def one_list(i, carry):
        which = step * SCATTER_LISTS + i
        count = row_ref[which, 2 * CAP]

        def one_group(g, c):
            for j in range(8):
                slot = g * 8 + j
                row = row_ref[which, slot]
                weight = rec_ref[which, CAP + slot]
                acc = accs[j % ACCS]
                acc[pl.ds(row, 1), :] = (
                    acc[pl.ds(row, 1), :] + wide_ref[pl.ds(i * CAP + slot, 1), :] * weight
                )
            return c

        lax.fori_loop(0, jnp.right_shift(count + 7, 3), one_group, 0)
        return carry

    lax.fori_loop(0, SCATTER_LISTS, one_list, 0)

    @pl.when(step == pl.num_programs(0) - 1)
    def _():
        def collect(i, total):
            at = pl.multiple_of(i * 64, 64)
            value = accs[0][pl.ds(at, 64), :]
            for acc in accs[1:]:
                value = value + acc[pl.ds(at, 64), :]
            out_ref[pl.ds(at, 64), :] = value
            square = value * value
            return total + jnp.sum(square.reshape(8, 8, TOK), axis=0)

        sq_ref[...] = lax.fori_loop(0, ROWS // 64, collect, jnp.zeros((8, TOK), F32))


def scatter_rows(row, record, cot):
    return pl.pallas_call(
        scatter_kernel,
        grid=(LISTS // SCATTER_LISTS,),
        in_specs=[
            pl.BlockSpec(memory_space=pltpu.SMEM),
            pl.BlockSpec(memory_space=pltpu.SMEM),
            pl.BlockSpec((SCATTER_LISTS * CAP, TOK), lambda g: (g, 0)),
        ],
        out_specs=(
            pl.BlockSpec((ROWS, TOK), lambda g: (0, 0)),
            pl.BlockSpec((8, TOK), lambda g: (0, 0)),
        ),
        out_shape=(
            jax.ShapeDtypeStruct((ROWS, TOK), F32),
            jax.ShapeDtypeStruct((8, TOK), F32),
        ),
        scratch_shapes=[pltpu.VMEM((SCATTER_LISTS * CAP, TOK), F32)]
        + [pltpu.VMEM((ROWS, TOK), F32) for _ in range(ACCS)],
        cost_estimate=pl.CostEstimate(
            flops=20_000_000_000, transcendentals=0, bytes_accessed=8_000_000
        ),
        name="scatter_rows",
    )(row, record, cot)


def dscore_kernel(ret_ref, aux_ref, out_ref):
    owner_id = lax.broadcasted_iota(jnp.int32, (TOK, TOK), 0)
    place_id = lax.broadcasted_iota(jnp.int32, (CAP, TOK), 0)
    for s in range(NDP):
        square = jnp.concatenate([ret_ref[:, s, :]] * 4, axis=0)
        columns = jnp.transpose(square)[0:CAP, :]
        parts = pieces(columns)
        target = aux_ref[s, 8:16, :].astype(jnp.int32)
        picked = []
        for k in range(PICKS):
            owner = jnp.right_shift(target[k : k + 1, :], 7)
            place = jnp.bitwise_and(target[k : k + 1, :], TOK - 1)
            chosen = jnp.where(owner_id == owner, 1.0, 0.0).astype(BF16)
            got = lax.dot_general(parts[0], chosen, NN, preferred_element_type=F32)
            got = got + lax.dot_general(parts[1], chosen, NN, preferred_element_type=F32)
            got = got + lax.dot_general(parts[2], chosen, NN, preferred_element_type=F32)
            picked.append(
                jnp.sum(jnp.where(place_id == place, got, 0.0), axis=0, keepdims=True)
            )
        picked = jnp.concatenate(picked, axis=0)
        weight = aux_ref[s, 0:8, :]
        both = weight * picked
        mean0 = jnp.sum(both[0:4, :], axis=0, keepdims=True)
        mean1 = jnp.sum(both[4:8, :], axis=0, keepdims=True)
        row = lax.broadcasted_iota(jnp.int32, (PICKS, TOK), 0)
        out_ref[s * 8 : s * 8 + 8, :] = weight * (picked - jnp.where(row < 4, mean0, mean1))


def partial_dscore(returned, aux):
    return pl.pallas_call(
        dscore_kernel,
        out_shape=jax.ShapeDtypeStruct((NDP * PICKS, TOK), F32),
        name="dscore",
    )(returned, aux)


def key_kernel(ds_ref, aux_ref, q_ref, base_ref, out_ref):
    dscore = ds_ref[0]
    for d in range(1, NDP):
        dscore = dscore + ds_ref[d]
    base = base_ref[0]
    key_id = lax.broadcasted_iota(jnp.int32, (KEYS, TOK), 0) + base
    for half in range(2):
        for head in range(2):
            at = head * 2 * HALF + half * HALF
            blocks = []
            for s in range(NDP):
                index = aux_ref[s, 16 + half * 8 : 24 + half * 8, :].astype(jnp.int32)
                block = jnp.zeros((KEYS, TOK), F32)
                for k in range(4):
                    slot = head * 4 + k
                    value = dscore[s * 8 + slot : s * 8 + slot + 1, :]
                    block = block + jnp.where(key_id == index[slot : slot + 1, :], value, 0.0)
                blocks.append(block)
            weighted = jnp.concatenate(blocks, axis=1)
            total = None
            for piece in pieces(weighted):
                term = lax.dot_general(
                    piece, q_ref[:, at : at + HALF], NN, preferred_element_type=F32
                )
                total = term if total is None else total + term
            out_ref[half, head] = total


def key_terms(dscore, aux, queries, base):
    return pl.pallas_call(
        key_kernel,
        in_specs=[
            pl.BlockSpec(memory_space=pltpu.VMEM),
            pl.BlockSpec(memory_space=pltpu.VMEM),
            pl.BlockSpec(memory_space=pltpu.VMEM),
            pl.BlockSpec(memory_space=pltpu.SMEM),
        ],
        out_shape=jax.ShapeDtypeStruct((2, 2, KEYS, HALF), F32),
        name="key_terms",
    )(dscore, aux, queries, base)


def exchange(x, axis):
    return lax.all_to_all(x, axis, 0, 0, tiled=True)


def everyone(x, axis, size):
    return exchange(jnp.broadcast_to(x[None], (size, *x.shape)), axis)


def local(queries, sub_keys, values, slot_first, slot_second, cotangent):
    q = queries.reshape(TOK, 4 * HALF)
    first = slot_first.reshape(TOK, PICKS).T
    second = slot_second.reshape(TOK, PICKS).T
    cot_columns = exchange(
        jnp.moveaxis(cotangent.reshape(TOK, NDP, TOK), 1, 0), "dp"
    )
    record, aux = prep(q, sub_keys, first, second)
    gathered = everyone(jnp.concatenate([record, aux], axis=0), "dp", NDP)
    records = gathered[:, 0:OWN, :]
    aux_all = gathered[:, OWN:, :]
    received = exchange(jnp.moveaxis(records, 1, 0), TABLE)
    rows = exchange(expand(records, cot_columns), TABLE)
    q_late, _ = lax.optimization_barrier((q, gathered))
    q_all = everyone(q_late, "dp", NDP).reshape(NDP * TOK, 4 * HALF)
    record_mine = received.reshape(LISTS, TOK)
    code = record_mine.astype(jnp.int32)
    lane = lax.broadcasted_iota(jnp.int32, (LISTS, TOK), 1)
    row = jnp.where(lane < CAP, jnp.right_shift(code, 7), code)
    value_rows = gather_rows(row, values.reshape(ROWS, TOK))
    rows_flat = rows.reshape(LISTS * CAP, TOK)
    partial = dots(rows_flat, value_rows)
    returned = exchange(partial.reshape(OWN, NDP, TOK), TABLE)
    value_grad, value_sq = scatter_rows(row, record_mine, rows_flat)
    dscore = everyone(partial_dscore(returned, aux_all), "dp", NDP)
    base = (lax.axis_index("dp") * KEYS).astype(jnp.int32).reshape(1)
    key_grad = key_terms(dscore, aux_all, q_all, base)
    key_blocks = jnp.moveaxis(key_grad.reshape(2, 2, OWN, 2, HALF), 2, 0)
    key_part = jnp.sum(exchange(key_blocks.reshape(OWN, 8, HALF), TABLE), axis=0)
    local_sq = jnp.sum(value_sq) + jnp.sum(key_part * key_part)
    total_sq = jnp.sum(everyone(local_sq.reshape(1), ALL, OWN * NDP))
    clip_factor = jnp.minimum(1.0, LIMIT_RATIO * math.sqrt(TOK * OWN * NDP) / jnp.sqrt(total_sq))
    value_update = (clip_factor * value_grad).reshape(BLK, NSUB, TOK)
    key_update = (clip_factor * key_part).reshape(2, 2, 2, HALF)
    return (value_update, key_update, clip_factor.reshape(1))


def solution(mesh):
    torus = Mesh(
        mesh.devices.reshape(mesh.shape["dp"], 4, 4, 2), ("dp", "table_0", "table_1", "table_2")
    )
    return jax.shard_map(
        local,
        mesh=torus,
        in_specs=(
            P(DP_TABLE, None, None),
            P(),
            P(TABLE, None, "dp"),
            P(DP_TABLE, None, None),
            P(DP_TABLE, None, None),
            P(DP_TABLE, None),
        ),
        out_specs=(P(TABLE, None, "dp"), P(None, None, DP_TABLE, None), P()),
        check_vma=False,
    )
```

time: 446 us -> 310 us (0.70)
  local copies, waits for them, and re-layouts: 153 us -> 14.5 us
  other arithmetic: 111 us -> 8.69 us
  Pallas kernels: 0 us -> 96 us
  waiting for transfers between devices: 56.3 us -> 100 us
  between operations: 17.8 us -> 3.88 us
  starting transfers between devices: 56.3 us -> 44.4 us
  blocking collectives: 45.9 us -> 39.9 us
    gather x7 -> x0, local copies, waits for them, and re-layouts: 115 us -> none  [the longest x1 45.9 us: local(): cot_part = cot_all[position.reshape(-1)]]
    pallas_call x0 -> x7, Pallas kernels: none -> 96 us  [the longest x1 55.1 us: scatter_rows(): pl.pallas_call(scatter_kernel, grid=(LISTS // SCATTER_LISTS,), in_specs=[...]
    scatter-add x1 -> x0, other arithmetic: 75.1 us -> none  [local(): start.at[rows_flat].add(weight_flat[:, None] * cot_part.astype(jnp.float32))]
    all_to_all x10 -> x7, waiting for transfers between devices: 56.2 us -> 100 us  [exchange(): return lax.all_to_all(x, axis, 0, 0, tiled=True)]
    scatter x3 -> x0, local copies, waits for them, and re-layouts: 13 us -> none  [the longest x1 4.32 us: local(): send_weight = jnp.zeros((table_size * capacity,), jnp.float32).at[target]...]
    all_to_all x10 -> x7, starting transfers between devices: 56.3 us -> 44.4 us  [exchange(): return lax.all_to_all(x, axis, 0, 0, tiled=True)]
    another operation x4 -> x0, other arithmetic: 9.29 us -> none
    reduce_sum x9 -> x4, other arithmetic: 9.16 us -> 2.8 us  [the longest x2 1.89 us: local(): local_sq = jnp.sum(value_sq) + jnp.sum(key_part * key_part)]
  transfers between devices with their start and end apart: 11 -> 7, of which waited for: 7 -> 6; matrix products, arithmetic and copies ran while one was open for 43% -> 2% of each run, Pallas kernels for 0% -> 25%
where the time goes in v1:
time: 310 us; the launch traced here: 308 us
  waiting for transfers between devices  100 us (32%)
  Pallas kernels  96 us (31%)
  starting transfers between devices  44.4 us (14%)
  blocking collectives  39.9 us (13%)
  local copies, waits for them, and re-layouts  14.5 us (5%)
  other arithmetic  8.69 us (3%)
  between operations  3.88 us (1%)
    all_to_all x7, waiting for transfers between devices, exchange(): return lax.all_to_all(x, axis, 0, 0, tiled=True)  100 us
    pallas_call x1, Pallas kernels, scatter_rows(): pl.pallas_call(scatter_kernel, grid=(LISTS // SCATTER_LISTS,), in_specs=[...  55.1 us
    all_to_all x7, starting transfers between devices, exchange(): return lax.all_to_all(x, axis, 0, 0, tiled=True)  44.4 us
    all_to_all x2, blocking collectives, exchange(): return lax.all_to_all(x, axis, 0, 0, tiled=True)  39.9 us
    pallas_call x1, Pallas kernels, gather_rows(): pl.pallas_call(gather_kernel, grid=(LISTS // GATHER_LISTS,), in_specs=[pl...  15.9 us
    pallas_call x1, Pallas kernels, expand(): pl.pallas_call(expand_kernel, grid=(NDP,), in_specs=[pl.BlockSpec((1, OWN...  7.24 us
    pallas_call x1, Pallas kernels, dots(): pl.pallas_call(dots_kernel, grid=(LISTS // DOT_LISTS,), in_specs=[pl.Bloc...  7.05 us
  transfers between devices with their start and end apart: 7, of which 6 were waited for; matrix products, arithmetic and copies ran while one was open for 2% of the time, Pallas kernels for 25%

profile of v1, /device:TPU:1, one launch (start us, length us, event | category | flops | bytes accessed | tf_op | source)
XLA Modules:
  0.0 307.7 jit_solution(9163441976036830345)
XLA Ops:
  0.6 1.7 copy.30
  2.3 3.5 %prep.1 = (f32[32,128]{1,0:T(8,128)}, f32[32,128]{1,0:T(8,128)}) custom-call(bf16[128,1024]{1,0:T(8,128)(2,1)} %bitcast.30, bf16[2,2,512,256]{3,2,1,0:T(8,128)(2,1)} %keys_ref.1, s32[8,128]{1,0:T(8,128)} %bitcast.37, s32[8,128]{1,0:T(8,128)} %bitcast.38), custom_call_target="tpu_custom_call" | custom-call | tf_op jit(solution)/shard_map/prep/pallas_call | solution.py:112
  7.3 9.0 %all-to-all-start = ((f32[8,64,128]{2,1,0:T(8,128)}), f32[8,64,128]{2,1,0:T(8,128)S(1)}, u32[]{:S(2)}, u32[]{:S(2)}) async-start(f32[8,64,128]{2,1,0:T(8,128)} %broadcast_in_dim.8), calls=%async_computation | async-start | bytes 524288 | tf_op jit(solution)/shard_map/all_to_all | solution.py:381
  16.3 1.1 copy.24
  18.2 8.5 %all-to-all-done = f32[8,64,128]{2,1,0:T(8,128)S(1)} async-done(((f32[8,64,128]{2,1,0:T(8,128)}), f32[8,64,128]{2,1,0:T(8,128)S(1)}, u32[]{:S(2)}, u32[]{:S(2)}) %all-to-all-start) | async-done | bytes 262176 | tf_op jit(solution)/shard_map/all_to_all | solution.py:381
  26.8 3.4 %all-to-all-start.2 = ((bf16[8,128,128]{2,1,0:T(8,128)(2,1)}), bf16[8,128,128]{2,1,0:T(8,128)(2,1)S(1)}, u32[]{:S(2)}, u32[]{:S(2)}) async-start(bf16[8,128,128]{2,1,0:T(8,128)(2,1)} %bitcast.7), calls=%async_computation.2 | async-start | bytes 524288 | tf_op jit(solution)/shard_map/all_to_all | solution.py:381
  31.6 7.9 %all-to-all-done.2.cot_ref = bf16[8,128,128]{2,1,0:T(8,128)(2,1)S(1)} async-done(((bf16[8,128,128]{2,1,0:T(8,128)(2,1)}), bf16[8,128,128]{2,1,0:T(8,128)(2,1)S(1)}, u32[]{:S(2)}, u32[]{:S(2)}) %all-to-all-start.2) | async-done | bytes 262176 | tf_op jit(solution)/shard_map/all_to_all | solution.py:381
  39.6 10.5 %all-to-all-start.1 = ((f32[32,8,128]{2,1,0:T(8,128)}), f32[32,8,128]{2,1,0:T(8,128)S(1)}, u32[]{:S(2)}, u32[]{:S(2)}) async-start(f32[32,8,128]{2,1,0:T(8,128)} %copy.23), calls=%async_computation.1 | async-start | bytes 262144 | tf_op jit(solution)/shard_map/all_to_all | solution.py:381
  50.0 7.2 %expand.1 = bf16[32,8,48,128]{3,2,1,0:T(8,128)(2,1)} custom-call(f32[8,32,128]{2,1,0:T(8,128)} %get-tuple-element.15.rec_ref, bf16[8,128,128]{2,1,0:T(8,128)(2,1)} %copy-done.4), custom_call_target="tpu_custom_call" | custom-call | tf_op jit(solution)/shard_map/expand/pallas_call | solution.py:137
  57.6 7.0 %all-to-all-start.3 = ((bf16[32,8,48,128]{3,2,1,0:T(8,128)(2,1)}), bf16[32,8,48,128]{3,2,1,0:T(8,128)(2,1)S(1)}, u32[]{:S(2)}, u32[]{:S(2)}) async-start(bf16[32,8,48,128]{3,2,1,0:T(8,128)(2,1)} %expand.1), calls=%async_computation.3 | async-start | bytes 6291456 | tf_op jit(solution)/shard_map/all_to_all | solution.py:381
  65.4 15.9 %gather_rows.1.value_ref = bf16[12288,128]{1,0:T(8,128)(2,1)} custom-call(s32[256,128]{1,0:T(8,128)} %shift-right-arithmetic_select_fusion.row_ref, bf16[8192,128]{1,0:T(8,128)(2,1)} %bitcast.39), custom_call_target="tpu_custom_call" | custom-call | flops 20000000000 | bytes 6000000 | tf_op jit(solution)/shard_map/gather_rows/pallas_call | solution.py:176
  81.2 23.2 %all-to-all-done.3 = bf16[32,8,48,128]{3,2,1,0:T(8,128)(2,1)S(1)} async-done(((bf16[32,8,48,128]{3,2,1,0:T(8,128)(2,1)}), bf16[32,8,48,128]{3,2,1,0:T(8,128)(2,1)S(1)}, u32[]{:S(2)}, u32[]{:S(2)}) %all-to-all-start.3) | async-done | bytes 3145760 | tf_op jit(solution)/shard_map/all_to_all | solution.py:381
  104.5 1.6 copy-done
  106.1 7.0 %dots.1 = f32[256,128]{1,0:T(8,128)} custom-call(bf16[12288,128]{1,0:T(8,128)(2,1)} %bitcast.26, bf16[12288,128]{1,0:T(8,128)(2,1)} %gather_rows.1.value_ref), custom_call_target="tpu_custom_call" | custom-call | tf_op jit(solution)/shard_map/dots/pallas_call | solution.py:211
  113.1 14.4 %all_to_all.46.ret_ref = f32[32,8,128]{2,1,0:T(8,128)} all-to-all(f32[32,8,128]{2,1,0:T(8,128)} %bitcast.34), channel_id=1, replica_groups=mesh['dp'=8,'table_0'=4,'table_1'=4,'table_2'=2] {'table_0','table_1','t..., dimensions={0} | all-to-all | bytes 262144 | tf_op jit(solution)/shard_map/all_to_all | solution.py:381
  127.5 3.4 %dscore.1 = f32[64,128]{1,0:T(8,128)} custom-call(f32[32,8,128]{2,1,0:T(8,128)} %all_to_all.46.ret_ref, f32[8,32,128]{2,1,0:T(8,128)} %get-tuple-element.13.aux_ref), custom_call_target="tpu_custom_call" | custom-call | tf_op jit(solution)/shard_map/dscore/pallas_call | solution.py:331
  130.9 1.5 broadcast_in_dim.9
  132.4 3.4 %all-to-all-start.5 = ((f32[8,64,128]{2,1,0:T(8,128)}), f32[8,64,128]{2,1,0:T(8,128)S(1)}, u32[]{:S(2)}, u32[]{:S(2)}) async-start(f32[8,64,128]{2,1,0:T(8,128)} %broadcast_in_dim.9), calls=%async_computation.5 | async-start | bytes 524288 | tf_op jit(solution)/shard_map/all_to_all | solution.py:381
  135.8 12.2 %all-to-all-done.5.ds_ref = f32[8,64,128]{2,1,0:T(8,128)S(1)} async-done(((f32[8,64,128]{2,1,0:T(8,128)}), f32[8,64,128]{2,1,0:T(8,128)S(1)}, u32[]{:S(2)}, u32[]{:S(2)}) %all-to-all-start.5) | async-done | bytes 262176 | tf_op jit(solution)/shard_map/all_to_all | solution.py:381
  148.0 1.6 broadcast_in_dim.10
  149.6 3.6 %all-to-all-start.6 = ((bf16[8,128,1024]{2,1,0:T(8,128)(2,1)}), bf16[8,128,1024]{2,1,0:T(8,128)(2,1)S(1)}, u32[]{:S(2)}, u32[]{:S(2)}) async-start(bf16[8,128,1024]{2,1,0:T(8,128)(2,1)} %broadcast_in_dim.10), calls=%async_computation.6 | async-start | bytes 4194304 | tf_op jit(solution)/shard_map/all_to_all | solution.py:381
  153.2 48.1 %all-to-all-done.6 = bf16[8,128,1024]{2,1,0:T(8,128)(2,1)S(1)} async-done(((bf16[8,128,1024]{2,1,0:T(8,128)(2,1)}), bf16[8,128,1024]{2,1,0:T(8,128)(2,1)S(1)}, u32[]{:S(2)}, u32[]{:S(2)}) %all-to-all-start.6) | async-done | bytes 2097184 | tf_op jit(solution)/shard_map/all_to_all | solution.py:381
  201.3 1.3 copy-done.1
  202.6 3.9 %key_terms.1 = f32[2,2,64,256]{3,2,1,0:T(8,128)} custom-call(f32[8,64,128]{2,1,0:T(8,128)} %copy-done.3, f32[8,32,128]{2,1,0:T(8,128)} %get-tuple-element.13.aux_ref, bf16[1024,1024]{1,0:T(8,128)(2,1)} %bitcast.28, s32[1]{0:T(128)} %bitcast.12.base_ref), custom_call_target="tpu_custom_call" | custom-call | tf_op jit(solution)/shard_map/key_terms/pallas_call | solution.py:367
  206.5 1.1 reshape.71
  207.6 0.9 copy.27
  208.5 7.5 %all-to-all-start.7 = ((f32[32,8,256]{2,1,0:T(8,128)}), f32[32,8,256]{2,1,0:T(8,128)S(1)}, u32[]{:S(2)}, u32[]{:S(2)}) async-start(f32[32,8,256]{2,1,0:T(8,128)} %copy.27), calls=%async_computation.7 | async-start | bytes 524288 | tf_op jit(solution)/shard_map/all_to_all | solution.py:381
  216.0 55.1 %scatter_rows.1 = (f32[8192,128]{1,0:T(8,128)}, f32[8,128]{1,0:T(8,128)}) custom-call(s32[256,128]{1,0:T(8,128)} %shift-right-arithmetic_select_fusion.row_ref, f32[256,128]{1,0:T(8,128)} %bitcast.35, bf16[12288,128]{1,0:T(8,128)(2,1)} %bitcast.27), custom_call_target="tpu_custom_call" | custom-call | flops 20000000000 | bytes 8000000 | tf_op jit(solution)/shard_map/scatter_rows/pallas_call | solution.py:277
  271.1 1.3 reduce_sum.36
  274.4 25.5 %all_to_all.47 = f32[256,1,1]{2,1,0:T(1,128)S(1)} all-to-all(f32[256,1,1]{2,1,0:T(1,128)S(1)} %broadcast_in_dim.11), channel_id=1, replica_groups=mesh['dp'=8,'table_0'=4,'table_1'=4,'table_2'=2] {'dp','table_0','table_..., dimensions={0} | all-to-all | bytes 2048 | tf_op jit(solution)/shard_map/all_to_all | solution.py:381
  299.9 0.9 reduce_sum.39
  302.1 4.5 %broadcast_multiply_fusion = f32[8192,128]{1,0:T(8,128)} fusion(f32[8192,128]{1,0:T(8,128)} %get-tuple-element.12, f32[]{:T(128)} %min_shard_map.3), kind=kLoop, calls=%fused_computation | loop fusion | flops 1048576 | bytes 8388612 | tf_op jit(solution)/shard_map/mul | solution.py:420
  (25 shorter events, 6.2 us)
Async XLA Ops:
  7.3 19.5 %all-to-all-start = ((f32[8,64,128]{2,1,0:T(8,128)}), f32[8,64,128]{2,1,0:T(8,128)S(1)}, u32[]{:S(2)}, u32[]{:S(2)}) async-start(f32[8,64,128]{2,1,0:T(8,128)} %broadcast_in_dim.8), calls=%async_computation | async-start | bytes 524288 | tf_op jit(solution)/shard_map/all_to_all | solution.py:381
  26.8 12.8 %all-to-all-start.2 = ((bf16[8,128,128]{2,1,0:T(8,128)(2,1)}), bf16[8,128,128]{2,1,0:T(8,128)(2,1)S(1)}, u32[]{:S(2)}, u32[]{:S(2)}) async-start(bf16[8,128,128]{2,1,0:T(8,128)(2,1)} %bitcast.7), calls=%async_computation.2 | async-start | bytes 524288 | tf_op jit(solution)/shard_map/all_to_all | solution.py:381
  39.6 10.5 %copy-start.4 = (bf16[8,128,128]{2,1,0:T(8,128)(2,1)}, bf16[8,128,128]{2,1,0:T(8,128)(2,1)S(1)}, u32[]{:S(2)}) copy-start(bf16[8,128,128]{2,1,0:T(8,128)(2,1)S(1)} %all-to-all-done.2.cot_ref) | copy-start | bytes 786436
  39.6 18.1 %all-to-all-start.1 = ((f32[32,8,128]{2,1,0:T(8,128)}), f32[32,8,128]{2,1,0:T(8,128)S(1)}, u32[]{:S(2)}, u32[]{:S(2)}) async-start(f32[32,8,128]{2,1,0:T(8,128)} %copy.23), calls=%async_computation.1 | async-start | bytes 262144 | tf_op jit(solution)/shard_map/all_to_all | solution.py:381
  57.6 7.1 %copy-start.5 = (f32[32,8,128]{2,1,0:T(8,128)}, f32[32,8,128]{2,1,0:T(8,128)S(1)}, u32[]{:S(2)}) copy-start(f32[32,8,128]{2,1,0:T(8,128)S(1)} %all-to-all-done.1) | copy-start | bytes 393220
  57.6 46.8 %all-to-all-start.3 = ((bf16[32,8,48,128]{3,2,1,0:T(8,128)(2,1)}), bf16[32,8,48,128]{3,2,1,0:T(8,128)(2,1)S(1)}, u32[]{:S(2)}, u32[]{:S(2)}) async-start(bf16[32,8,48,128]{3,2,1,0:T(8,128)(2,1)} %expand.1), calls=%async_computation.3 | async-start | bytes 6291456 | tf_op jit(solution)/shard_map/all_to_all | solution.py:381
  104.5 1.6 copy-start
  106.1 42.0 %copy-start.2 = (bf16[16,8,2,512]{3,1,2,0:T(8,128)(2,1)S(1)}, bf16[16,8,2,512]{3,1,2,0:T(8,128)(2,1)}, u32[]{:S(2)}) copy-start(bf16[16,8,2,512]{3,1,2,0:T(8,128)(2,1)} %copy.30) | copy-start | bytes 786436
  132.4 15.6 %all-to-all-start.5 = ((f32[8,64,128]{2,1,0:T(8,128)}), f32[8,64,128]{2,1,0:T(8,128)S(1)}, u32[]{:S(2)}, u32[]{:S(2)}) async-start(f32[8,64,128]{2,1,0:T(8,128)} %broadcast_in_dim.9), calls=%async_computation.5 | async-start | bytes 524288 | tf_op jit(solution)/shard_map/all_to_all | solution.py:381
  148.0 1.6 copy-start.3
  149.6 51.7 %all-to-all-start.6 = ((bf16[8,128,1024]{2,1,0:T(8,128)(2,1)}), bf16[8,128,1024]{2,1,0:T(8,128)(2,1)S(1)}, u32[]{:S(2)}, u32[]{:S(2)}) async-start(bf16[8,128,1024]{2,1,0:T(8,128)(2,1)} %broadcast_in_dim.10), calls=%async_computation.6 | async-start | bytes 4194304 | tf_op jit(solution)/shard_map/all_to_all | solution.py:381
  201.3 1.3 copy-start.1
  208.5 63.9 %all-to-all-start.7 = ((f32[32,8,256]{2,1,0:T(8,128)}), f32[32,8,256]{2,1,0:T(8,128)S(1)}, u32[]{:S(2)}, u32[]{:S(2)}) async-start(f32[32,8,256]{2,1,0:T(8,128)} %copy.27), calls=%async_computation.7 | async-start | bytes 524288 | tf_op jit(solution)/shard_map/all_to_all | solution.py:381
